TPU v7x, 256 devices: a whole 4x4x8 slice. The times are simulated.
256 devices in a mesh: row: 16 (over x, z_lo), col: 16 (over y, z_hi, core).
Axes of the slice: x: 4, y: 4, z: 8 (z_hi: 2, z_lo: 4; z = z_hi * 4 + z_lo), core: 2. Of those that a mesh axis runs over, the one named last changes fastest.
Arguments:
- t2_amps: bfloat16 [16384, 49152], P('row', 'col'), may hold values from -0.5 to 0.5
- l2_amps: bfloat16 [512, 49152], P('row', 'col'), may hold values from -0.02734375 to 0.02734375
Outputs:
- ladder: bfloat16 [512, 49152], P('row', 'col')
All inputs are finite; a program needn't handle non-finite values.
Results may differ from a plain program's by a relative error of at most 0.0044.
Values may be sent and summed in bfloat16 or wider, within the bound.
No kernel may reach another device: no remote copies, remote signals or barrier semaphores. Data moves between devices by JAX's collectives and lax.ppermute only.
A program may use at most 64 MiB of HBM per device.

v0:
```python
import jax
import jax.numpy as jnp
from jax import lax
from jax.sharding import Mesh
from jax.sharding import PartitionSpec as P

ROW = ("row_0", "row_1")
COL = ("col_0", "col_1", "col_2")


def in_blocks(value, dim, size):
    dims = value.shape
    parts = value.reshape(*dims[:dim], size, dims[dim] // size, *dims[dim + 1 :])
    return jnp.moveaxis(parts, dim, 0)


def sum_at_owner(value, axis, dim):
    parts = in_blocks(value, dim, lax.axis_size(axis))
    arrived = lax.all_to_all(parts, axis, split_axis=0, concat_axis=0, tiled=True)
    return arrived.sum(axis=0)


def sum_by_axis(value, axes, dim):
    far, near = axes
    own = sum_at_owner(in_blocks(value, dim, lax.axis_size(far)), near, dim + 1)
    return jnp.sum(lax.all_to_all(own, far, 0, 0, tiled=True), axis=0)


def padded_to(lines, size):
    spare = -lines.shape[0] % size
    if not spare:
        return lines
    return jnp.concatenate([lines, jnp.zeros((spare, *lines.shape[1:]), lines.dtype)])


def from_everyone(value, axis):
    size = lax.axis_size(axis)
    return lax.all_to_all(
        jnp.broadcast_to(value[None], (size, *value.shape)), axis, 0, 0, tiled=True
    )


def in_order(parts, dim):
    dims = list(parts.shape[1:])
    dims[dim] *= parts.shape[0]
    return jnp.moveaxis(parts, 0, dim).reshape(dims)


def gather_axes(value, axes, dim):
    far, near = axes
    initial = from_everyone(value, far)
    parts = jnp.swapaxes(from_everyone(initial, near), 0, 1)
    return in_order(parts.reshape(-1, *value.shape), dim)


def sum_by_parts(value, axes):
    lines = value.reshape(-1, value.shape[-1])
    own = sum_by_axis(padded_to(lines, lax.axis_size(axes[0]) * lax.axis_size(axes[1])), axes, 0)
    whole = gather_axes(own, axes, 0)
    return whole[: len(lines)].reshape(value.shape)


def own_rows(subtotal, axes):
    for axis in axes:
        subtotal = lax.psum_scatter(subtotal, axis, scatter_dimension=0, tiled=True)
    return subtotal


def on_device(t2_amps, l2_amps):
    partial_value = jnp.dot(
        t2_amps,
        lax.all_gather(l2_amps, ROW, axis=0, tiled=True).T,
        preferred_element_type=jnp.float32,
    )
    oooo = sum_by_parts(partial_value, (("col_0", "col_1"), "col_2"))
    oooo_half = oooo.astype(jnp.bfloat16)
    ladder = own_rows(
        lax.dot_general(
            oooo_half, t2_amps, (((0,), (0,)), ((), ())), preferred_element_type=jnp.float32
        ),
        ROW,
    )
    return ladder.astype(jnp.bfloat16)


def solution(mesh):
    finer = Mesh(mesh.devices.reshape(4, 4, 4, 2, 2), ("row_0", "row_1", "col_0", "col_1", "col_2"))
    return jax.shard_map(
        on_device,
        mesh=finer,
        in_specs=(P(ROW, COL), P(ROW, COL)),
        out_specs=P(ROW, COL),
        check_vma=False,
    )
```

profile of v0, /device:TPU:1, one launch (start us, length us, event | category | flops | bytes accessed | tf_op | source)
XLA Modules:
  0.0 296.4 jit_solution(4271393291127959320)
XLA Ops:
  6.5 0.0 all-gather.2.cloned.1.call-start
  6.5 0.7 all-gather.2.cloned.1.call-update
  7.3 0.0 reduce-scatter.3.cloned.1.call-start
  7.3 87.6 %all-gather.2.cloned.1.call-done = bf16[512,3072]{1,0:T(8,128)(2,1)} async-done(((bf16[32,3072]{1,0:T(8,128)(2,1)}), bf16[512,3072]{1,0:T(8,128)(2,1)}) %all-gather.2.cloned.1.call-update) | async-done | bytes 3145744 | tf_op jit(solution)/shard_map/all_gather | solution.py:72
  94.9 6.5 %fusion = f32[1024,512]{1,0:T(8,128)S(1)} fusion(bf16[1024,3072]{1,0:T(8,128)(2,1)} %param.2, bf16[512,3072]{1,0:T(8,128)(2,1)} %all-gather.2.cloned.1.call-done), kind=kOutput, calls=%fused_computation.2 | convolution fusion | flops 3221225472 | bytes 11534336 | tf_op jit(solution)/shard_map/dot_general | solution.py:70
  101.4 0.2 copy.10
  101.7 15.1 %all_to_all.20 = f32[2,8,64,512]{3,2,1,0:T(8,128)S(1)} all-to-all(f32[2,8,64,512]{3,2,1,0:T(8,128)S(1)} %bitcast.11), channel_id=1, replica_groups=mesh['row_0'=4,'row_1'=4,'col_0'=4,'col_1'=2,'col_2'=2] {'col_2'}, dimensions={0} | all-to-all | bytes 4194304 | tf_op jit(solution)/shard_map/all_to_all | solution.py:19
  116.8 0.3 reduce_sum.18
  117.1 33.2 %all_to_all.21 = f32[8,64,512]{2,1,0:T(8,128)S(1)} all-to-all(f32[8,64,512]{2,1,0:T(8,128)S(1)} %reduce_sum.18), channel_id=1, replica_groups=mesh['row_0'=4,'row_1'=4,'col_0'=4,'col_1'=2,'col_2'=2] {'col_0','col_1'}, dimensions={0} | all-to-all | bytes 2097152 | tf_op jit(solution)/shard_map/all_to_all | solution.py:26
  150.3 0.1 reduce_sum.19
  150.5 17.2 %all_to_all.22 = bf16[8,64,512]{2,1,0:T(8,128)(2,1)S(1)} all-to-all(bf16[8,64,512]{2,1,0:T(8,128)(2,1)S(1)} %broadcast_in_dim.4), channel_id=1, replica_groups=mesh['row_0'=4,'row_1'=4,'col_0'=4,'col_1'=2,'col_2'=2] {'col_0','col_1'}, dimensions={0} | all-to-all | bytes 1048576 | tf_op jit(solution)/shard_map/all_to_all | solution.py:38
  167.7 0.1 broadcast_in_dim.5
  167.8 7.5 %all_to_all.23 = bf16[2,8,64,512]{3,2,1,0:T(8,128)(2,1)S(1)} all-to-all(bf16[2,8,64,512]{3,2,1,0:T(8,128)(2,1)S(1)} %broadcast_in_dim.5), channel_id=1, replica_groups=mesh['row_0'=4,'row_1'=4,'col_0'=4,'col_1'=2,'col_2'=2] {'col_2'}, dimensions={0} | all-to-all | bytes 2097152 | tf_op jit(solution)/shard_map/all_to_all | solution.py:38
  175.3 0.1 copy.9
  175.4 8.2 %fusion.1 = f32[512,3072]{1,0:T(8,128)} fusion(bf16[1024,512]{1,0:T(8,128)(2,1)S(1)} %bitcast.12, bf16[1024,3072]{1,0:T(8,128)(2,1)} %param.2), kind=kOutput, calls=%fused_computation.3 | convolution fusion | flops 3221225472 | bytes 13631488 | tf_op jit(solution)/shard_map/dot_general | solution.py:78
  183.6 0.0 reduce-scatter.3.cloned.1.call-update
  183.6 0.0 reduce-scatter.5.cloned.1.call-start
  183.7 61.7 %reduce-scatter.3.cloned.1.call-done = f32[128,3072]{1,0:T(8,128)} async-done(((f32[512,3072]{1,0:T(8,128)}), f32[128,3072]{1,0:T(8,128)}) %reduce-scatter.3.cloned.1.call-update) | async-done | bytes 1572880 | tf_op jit(solution)/shard_map/reduce_scatter | solution.py:65
  245.4 0.0 reduce-scatter.5.cloned.1.call-update
  245.4 42.7 %reduce-scatter.5.cloned.1.call-done = f32[32,3072]{1,0:T(8,128)} async-done(((f32[128,3072]{1,0:T(8,128)}), f32[32,3072]{1,0:T(8,128)}) %reduce-scatter.5.cloned.1.call-update) | async-done | bytes 393232 | tf_op jit(solution)/shard_map/reduce_scatter | solution.py:65
  288.1 1.7 convert_element_type.15
  (1 shorter events, 0.0 us)
Async XLA Ops:
  6.5 88.4 %all-gather.2.cloned.1.call-start = ((), (), s32[]{:S(2)}) async-start(), calls=%async_computation.6 | async-start | bytes 3342336 | tf_op jit(solution)/shard_map/all_gather | solution.py:72
  7.3 238.1 %reduce-scatter.3.cloned.1.call-start = ((), (), s32[]{:S(2)}) async-start(), calls=%async_computation.7 | async-start | bytes 7864320 | tf_op jit(solution)/shard_map/reduce_scatter | solution.py:65
  183.6 104.5 %reduce-scatter.5.cloned.1.call-start = ((), (), s32[]{:S(2)}) async-start(), calls=%async_computation.8 | async-start | bytes 1966080 | tf_op jit(solution)/shard_map/reduce_scatter | solution.py:65
Sparse Core Ops, SparseCore 0:
  9.1 85.7 all-gather.1
  183.7 61.5 reduce-scatter.2
  247.9 40.1 reduce-scatter.4
where the time goes:
time: 297 us; the launch traced here: 296 us
  waiting for transfers between devices  193 us (65%)
  blocking collectives  73.1 us (25%)
  matrix products  14.7 us (5%)
  between operations  13.2 us (4%)
    reduce_scatter x2, waiting for transfers between devices, own_rows(): subtotal = lax.psum_scatter(subtotal, axis, scatter_dimension=0, tiled=True)  104 us
    all_gather x1, waiting for transfers between devices, on_device(): lax.all_gather(l2_amps, ROW, axis=0, tiled=True)  87.6 us
    all_to_all x1, blocking collectives, sum_by_axis(): return jnp.sum(lax.all_to_all(own, far, 0, 0, tiled=True), axis=0)  33.2 us
    all_to_all x2, blocking collectives, from_everyone(): lax.all_to_all(jnp.broadcast_to(value[None], (size, *value.shape)), axis,...  24.8 us
    all_to_all x1, blocking collectives, sum_at_owner(): lax.all_to_all(parts, axis, split_axis=0, concat_axis=0, tiled=True)  15.1 us
    dot_general x1, matrix products, on_device(): lax.dot_general(oooo_half, t2_amps, (((0,), (0,)), ((), ())), preferred_e...  8.19 us
    dot_general x1, matrix products, on_device(): jnp.dot(t2_amps, lax.all_gather(l2_amps, ROW, axis=0, tiled=True).T, pref...  6.51 us
  transfers between devices with their start and end apart: 3, of which 3 were waited for; matrix products, arithmetic and copies ran while one was open for 0% of the time, Pallas kernels for 0%

commit v1 on v0

--- a/solution.py
+++ b/solution.py
@@ -69,7 +69,9 @@
 def on_device(t2_amps, l2_amps):
     partial_value = jnp.dot(
         t2_amps,
-        lax.all_gather(l2_amps, ROW, axis=0, tiled=True).T,
+        jnp.concatenate(
+            lax.all_to_all(jnp.stack([l2_amps] * lax.axis_size(ROW)), ROW, 0, 0), axis=0
+        ).T,
         preferred_element_type=jnp.float32,
     )
     oooo = sum_by_parts(partial_value, (("col_0", "col_1"), "col_2"))

time: 297 us -> 282 us (0.949)
  waiting for transfers between devices: 193 us -> 104 us
  blocking collectives: 73.1 us -> 148 us
  matrix products: 14.7 us -> 11.6 us
    all_gather x1 -> x0, waiting for transfers between devices: 87.6 us -> none  [on_device(): lax.all_gather(l2_amps, ROW, axis=0, tiled=True)]
    all_to_all x0 -> x1, blocking collectives: none -> 81 us  [on_device(): lax.all_to_all(jnp.stack([l2_amps] * lax.axis_size(ROW)), ROW, 0, 0)]
    all_to_all x1, blocking collectives: 15.1 us -> 6.73 us  [sum_at_owner(): lax.all_to_all(parts, axis, split_axis=0, concat_axis=0, tiled=True)]
    dot_general x1, matrix products: 6.51 us -> 3.44 us  [on_device(): jnp.dot(t2_amps, jnp.concatenate(lax.all_to_all(jnp.stack([l2_amps] * lax...]
  transfers between devices with their start and end apart: 3 -> 2, of which waited for: 3 -> 2; matrix products, arithmetic and copies ran while one was open for 0% -> 0% of each run, Pallas kernels for 0% -> 0%
where the time goes in v1:
time: 282 us; the launch traced here: 281 us
  blocking collectives  148 us (52%)
  waiting for transfers between devices  104 us (37%)
  between operations  13.5 us (5%)
  matrix products  11.6 us (4%)
    reduce_scatter x2, waiting for transfers between devices, own_rows(): subtotal = lax.psum_scatter(subtotal, axis, scatter_dimension=0, tiled=True)  104 us
    all_to_all x1, blocking collectives, on_device(): lax.all_to_all(jnp.stack([l2_amps] * lax.axis_size(ROW)), ROW, 0, 0)  81 us
    all_to_all x1, blocking collectives, sum_by_axis(): return jnp.sum(lax.all_to_all(own, far, 0, 0, tiled=True), axis=0)  35.7 us
    all_to_all x2, blocking collectives, from_everyone(): lax.all_to_all(jnp.broadcast_to(value[None], (size, *value.shape)), axis,...  24.8 us
    dot_general x1, matrix products, on_device(): lax.dot_general(oooo_half, t2_amps, (((0,), (0,)), ((), ())), preferred_e...  8.19 us
    all_to_all x1, blocking collectives, sum_at_owner(): lax.all_to_all(parts, axis, split_axis=0, concat_axis=0, tiled=True)  6.73 us
  transfers between devices with their start and end apart: 2, of which 2 were waited for; matrix products, arithmetic and copies ran while one was open for 0% of the time, Pallas kernels for 0%

profile of v1, /device:TPU:1, one launch (start us, length us, event | category | flops | bytes accessed | tf_op | source)
XLA Modules:
  0.0 281.2 jit_solution(8237848987299480635)
XLA Ops:
  6.5 0.0 reduce-scatter.3.cloned.1.call-start
  6.5 1.3 stack.2
  7.8 0.0 copy-start
  7.9 81.0 %all_to_all.25 = bf16[16,32,3072]{2,1,0:T(8,128)(2,1)S(1)} all-to-all(bf16[16,32,3072]{2,1,0:T(8,128)(2,1)S(1)} %stack.2), channel_id=1, replica_groups=mesh['row_0'=4,'row_1'=4,'col_0'=4,'col_1'=2,'col_2'=2] {'row_0','row_1'}, dimensions={0} | all-to-all | bytes 6291456 | tf_op jit(solution)/shard_map/all_to_all | solution.py:73
  88.9 0.0 copy-done
  88.9 3.4 %convolution_bitcast_fusion = f32[2,8,64,512]{3,2,0,1:T(8,128)S(1)} fusion(bf16[8,2,64,3072]{3,2,1,0:T(8,128)(2,1)S(1)} %bitcast.15, bf16[512,3072,1,1]{1,0,3,2:T(8,128)(2,1)S(1)} %bitcast.17), kind=kOutput, calls=%fused_computation.1 | convolution fusion | flops 3221225472 | bytes 11534336 | tf_op jit(solution)/shard_map/dot_general | solution.py:70
  92.3 0.2 copy.5
  92.5 6.7 %all_to_all.26 = f32[2,8,64,512]{3,2,1,0:T(8,128)S(1)} all-to-all(f32[2,8,64,512]{3,2,1,0:T(8,128)S(1)} %copy.5), channel_id=1, replica_groups=mesh['row_0'=4,'row_1'=4,'col_0'=4,'col_1'=2,'col_2'=2] {'col_2'}, dimensions={0} | all-to-all | bytes 4194304 | tf_op jit(solution)/shard_map/all_to_all | solution.py:19
  99.3 0.3 reduce_sum.18
  99.6 35.7 %all_to_all.27 = f32[8,64,512]{2,1,0:T(8,128)S(1)} all-to-all(f32[8,64,512]{2,1,0:T(8,128)S(1)} %reduce_sum.18), channel_id=1, replica_groups=mesh['row_0'=4,'row_1'=4,'col_0'=4,'col_1'=2,'col_2'=2] {'col_0','col_1'}, dimensions={0} | all-to-all | bytes 2097152 | tf_op jit(solution)/shard_map/all_to_all | solution.py:26
  135.2 0.1 reduce_sum.19
  135.3 18.8 %all_to_all.28 = bf16[8,64,512]{2,1,0:T(8,128)(2,1)S(1)} all-to-all(bf16[8,64,512]{2,1,0:T(8,128)(2,1)S(1)} %broadcast_in_dim.4), channel_id=1, replica_groups=mesh['row_0'=4,'row_1'=4,'col_0'=4,'col_1'=2,'col_2'=2] {'col_0','col_1'}, dimensions={0} | all-to-all | bytes 1048576 | tf_op jit(solution)/shard_map/all_to_all | solution.py:38
  154.2 0.1 broadcast_in_dim.5
  154.3 6.0 %all_to_all.29 = bf16[2,8,64,512]{3,2,1,0:T(8,128)(2,1)S(1)} all-to-all(bf16[2,8,64,512]{3,2,1,0:T(8,128)(2,1)S(1)} %broadcast_in_dim.5), channel_id=1, replica_groups=mesh['row_0'=4,'row_1'=4,'col_0'=4,'col_1'=2,'col_2'=2] {'col_2'}, dimensions={0} | all-to-all | bytes 2097152 | tf_op jit(solution)/shard_map/all_to_all | solution.py:38
  160.3 0.1 copy.9
  160.4 8.2 %fusion = f32[512,3072]{1,0:T(8,128)} fusion(bf16[1024,512]{1,0:T(8,128)(2,1)S(1)} %bitcast.16, bf16[1024,3072]{1,0:T(8,128)(2,1)} %param.2), kind=kOutput, calls=%fused_computation.2 | convolution fusion | flops 3221225472 | bytes 13631488 | tf_op jit(solution)/shard_map/dot_general | solution.py:80
  168.5 0.0 reduce-scatter.3.cloned.1.call-update
  168.6 0.0 reduce-scatter.5.cloned.1.call-start
  168.6 61.3 %reduce-scatter.3.cloned.1.call-done = f32[128,3072]{1,0:T(8,128)} async-done(((f32[512,3072]{1,0:T(8,128)}), f32[128,3072]{1,0:T(8,128)}) %reduce-scatter.3.cloned.1.call-update) | async-done | bytes 1572880 | tf_op jit(solution)/shard_map/reduce_scatter | solution.py:65
  230.0 0.0 reduce-scatter.5.cloned.1.call-update
  230.0 42.7 %reduce-scatter.5.cloned.1.call-done = f32[32,3072]{1,0:T(8,128)} async-done(((f32[128,3072]{1,0:T(8,128)}), f32[32,3072]{1,0:T(8,128)}) %reduce-scatter.5.cloned.1.call-update) | async-done | bytes 393232 | tf_op jit(solution)/shard_map/reduce_scatter | solution.py:65
  272.7 1.7 convert_element_type.15
  (1 shorter events, 0.0 us)
Async XLA Ops:
  6.5 223.4 %reduce-scatter.3.cloned.1.call-start = ((), (), s32[]{:S(2)}) async-start(), calls=%async_computation.7 | async-start | bytes 7864320 | tf_op jit(solution)/shard_map/reduce_scatter | solution.py:65
  7.8 81.0 %copy-start = (bf16[1024,3072]{1,0:T(8,128)(2,1)S(1)}, bf16[1024,3072]{1,0:T(8,128)(2,1)}, u32[]{:S(2)}) copy-start(bf16[1024,3072]{1,0:T(8,128)(2,1)} %param.2) | copy-start | bytes 18874372
  168.6 104.1 %reduce-scatter.5.cloned.1.call-start = ((), (), s32[]{:S(2)}) async-start(), calls=%async_computation.8 | async-start | bytes 1966080 | tf_op jit(solution)/shard_map/reduce_scatter | solution.py:65
Sparse Core Ops, SparseCore 0:
  168.7 61.2 reduce-scatter.2
  232.5 40.1 reduce-scatter.4
